TPU v7x, 32 devices: a whole 2x2x4 slice. The times are simulated.
32 devices in a mesh: vert: 8 (over z, y), col: 4 (over x, core).
Axes of the slice: x: 2, y: 2, z: 4, core: 2. Of those that a mesh axis runs over, the one named last changes fastest.
Arguments:
- coeffs: bfloat16 [64, 400], P(('vert', 'col')), may hold values from -6 to 6
- shape_basis: bfloat16 [400, 3, 656], P('col', None, 'vert'), may hold values from -0.3125 to 0.3125
- template: float32 [3, 656], P(None, 'vert'), may hold values from -6 to 6
- regressor: float32 [55, 656], P(None, 'vert'), may hold values from -0.5 to 0.5
- quaternions: float32 [64, 4, 55], P(('vert', 'col')), may hold values from -1.5 to 1.5, as said below
- translation: float32 [64, 3], P(('vert', 'col')), may hold values from -6 to 6
- parents: int32 [55], replicated, may hold values from 0 to 53, as said below
- skin_index: int32 [656, 4], P('vert'), may hold values from 0 to 54, all different within a row
- skin_raw: float32 [656, 4], P('vert'), may hold values from 0.1 to 1
Outputs:
- posed_vertices: bfloat16 [64, 3, 656], P(('vert', 'col'))
Inputs may be any that keep to these rules, and one draw needn't show every extreme that they name: parents[0] = 0 and parents[j] < j for j >= 1. `skin_index`: the four joints of a vertex differ. `quaternions`: component 0 lies in [0.5, 1.5].
All inputs are finite; a program needn't handle non-finite values.
Results may differ from a plain program's by a relative error of at most 0.0024.
Values may be sent and summed in bfloat16 or wider, within the bound.
No kernel may reach another device: no remote copies, remote signals or barrier semaphores. Data moves between devices by JAX's collectives and lax.ppermute only.
A program may use at most 64 MiB of HBM per device.

v0:
```python
import jax
import jax.numpy as jnp
from jax import lax
from jax.sharding import PartitionSpec as P


def rotations(quaternions):
    quat_w = jnp.transpose(quaternions[:, 0])
    quat_x = jnp.transpose(quaternions[:, 1])
    quat_y = jnp.transpose(quaternions[:, 2])
    quat_z = jnp.transpose(quaternions[:, 3])
    scale_two = 2.0 / (quat_w * quat_w + quat_x * quat_x + quat_y * quat_y + quat_z * quat_z)
    matrix_rows = [
        [
            1.0 - scale_two * (quat_y * quat_y + quat_z * quat_z),
            scale_two * (quat_x * quat_y - quat_w * quat_z),
            scale_two * (quat_x * quat_z + quat_w * quat_y),
        ],
        [
            scale_two * (quat_x * quat_y + quat_w * quat_z),
            1.0 - scale_two * (quat_x * quat_x + quat_z * quat_z),
            scale_two * (quat_y * quat_z - quat_w * quat_x),
        ],
        [
            scale_two * (quat_x * quat_z - quat_w * quat_y),
            scale_two * (quat_y * quat_z + quat_w * quat_x),
            1.0 - scale_two * (quat_x * quat_x + quat_y * quat_y),
        ],
    ]
    return jnp.stack([jnp.stack(entry, axis=1) for entry in matrix_rows], axis=1)


def kinematics(joints, quaternions, translation, parents):
    joint_total = quaternions.shape[2]
    local_rots = rotations(quaternions)
    places = jnp.transpose(joints, (2, 1, 0))
    glob_rot = jnp.zeros_like(local_rots).at[0].set(local_rots[0])
    glob_pos = jnp.zeros_like(places).at[0].set(places[0] + jnp.transpose(translation))

    def compose(joint, state_pair):
        rot_now, pos_now = state_pair
        parent = lax.dynamic_index_in_dim(parents, joint, 0, keepdims=False)
        parent_rot = lax.dynamic_index_in_dim(rot_now, parent, 0, keepdims=False)
        parent_pos = lax.dynamic_index_in_dim(pos_now, parent, 0, keepdims=False)
        local_rot = lax.dynamic_index_in_dim(local_rots, joint, 0, keepdims=False)
        offset = lax.dynamic_index_in_dim(
            places, joint, 0, keepdims=False
        ) - lax.dynamic_index_in_dim(places, parent, 0, keepdims=False)
        new_rot = jnp.einsum("amc,mbc->abc", parent_rot, local_rot, precision=lax.Precision.HIGHEST)
        new_pos = (
            jnp.einsum("amc,mc->ac", parent_rot, offset, precision=lax.Precision.HIGHEST)
            + parent_pos
        )
        rot_now = lax.dynamic_update_index_in_dim(rot_now, new_rot, joint, 0)
        pos_now = lax.dynamic_update_index_in_dim(pos_now, new_pos, joint, 0)
        return (rot_now, pos_now)

    glob_rot, glob_pos = lax.fori_loop(1, joint_total, compose, (glob_rot, glob_pos))
    correction = glob_pos - jnp.einsum(
        "jamc,jmc->jac", glob_rot, places, precision=lax.Precision.HIGHEST
    )
    frames = jnp.concatenate(
        [glob_rot.reshape(joint_total, 9, glob_rot.shape[3]), correction], axis=1
    )
    return jnp.transpose(frames, (2, 1, 0))


def dense_weights(joint_index, raw_weights, joint_total):
    shares = raw_weights / jnp.sum(raw_weights, axis=1, keepdims=True)
    matches = joint_index[None, :, :] == jnp.arange(joint_total, dtype=jnp.int32)[:, None, None]
    return jnp.sum(
        jnp.where(matches, shares[None, :, :], jnp.zeros_like(shares)[None, :, :]), axis=2
    )


def apply_frames(blended, shaped_wide):
    coords = []
    for axis_out in range(3):
        value = blended[:, 9 + axis_out]
        for axis_in in range(3):
            value = value + blended[:, 3 * axis_out + axis_in] * shaped_wide[:, axis_in]
        coords.append(value)
    return jnp.stack(coords, axis=1)


def body(
    coeffs,
    shape_basis,
    template,
    regressor,
    quaternions,
    translation,
    parents,
    skin_index,
    skin_raw,
):
    joint_total = regressor.shape[0]
    full_basis = lax.all_gather(shape_basis, "col", axis=0, tiled=True)
    components = full_basis.shape[0]
    vert_count = full_basis.shape[2]
    flat_basis = full_basis.reshape(components, 3 * vert_count)
    base_row = template.reshape(1, 3 * vert_count)
    full_shape = (
        jnp.dot(
            lax.all_gather(coeffs, "vert", axis=0, tiled=True),
            flat_basis,
            preferred_element_type=jnp.float32,
        )
        + base_row
    )
    group_count = full_shape.shape[0]
    shaped_three = full_shape.astype(jnp.bfloat16).reshape(group_count, 3, vert_count)
    partial_value = jnp.einsum(
        "cmv,jv->cmj",
        full_shape.reshape(group_count, 3, vert_count),
        regressor,
        precision=lax.Precision.HIGHEST,
    )
    joints = lax.psum_scatter(partial_value, "vert", scatter_dimension=0, tiled=True)
    own_frames = kinematics(joints, quaternions, translation, parents)
    group_frames = lax.all_gather(own_frames, "vert", axis=0, tiled=True)
    weight_grid = dense_weights(skin_index, skin_raw, joint_total)
    blended = jnp.einsum("cej,jv->cev", group_frames, weight_grid, precision=lax.Precision.HIGHEST)
    posed_local = apply_frames(blended, shaped_three.astype(jnp.float32)).astype(jnp.bfloat16)
    return lax.all_to_all(posed_local, "vert", split_axis=0, concat_axis=2, tiled=True)


def solution(mesh):
    in_specs = (
        P(("vert", "col"), None),
        P("col", None, "vert"),
        P(None, "vert"),
        P(None, "vert"),
        P(("vert", "col"), None, None),
        P(("vert", "col"), None),
        P(),
        P("vert", None),
        P("vert", None),
    )
    out_specs = P(("vert", "col"), None, None)
    return jax.shard_map(body, mesh=mesh, in_specs=in_specs, out_specs=out_specs, check_vma=False)
```

profile of v0, /device:TPU:0, one launch (start us, length us, event | category | flops | bytes accessed | tf_op | source)
XLA Modules:
  0.0 288.7 jit_solution(18105276202222392193)
XLA Ops:
  0.0 0.9 multiply_add_fusion.2
  0.9 0.8 add.183
  1.7 28.1 %all-gather = bf16[8,2,400]{2,1,0:T(2,128)(2,1)S(1)} all-gather(bf16[1,2,400]{2,1,0:T(2,128)(2,1)} %bitcast.166), channel_id=1, replica_groups=mesh['vert'=8,'col'=4] {'vert'}, dimensions={0}, use_global_device_ids=true | all-gather | bytes 14400 | tf_op jit(solution)/shard_map/all_gather | solution.py:105
  29.9 6.5 %all_gather.10 = bf16[400,3,82]{2,1,0:T(4,128)(2,1)S(1)} all-gather(bf16[100,3,82]{2,1,0:T(4,128)(2,1)S(1)} %copy.86), channel_id=1, replica_groups=mesh['vert'=8,'col'=4] {'col'}, dimensions={0}, use_global_device_ids=true | all-gather | bytes 246000 | tf_op jit(solution)/shard_map/all_gather | solution.py:98
  38.1 35.4 %all-reduce.1 = f32[16,3,55]{2,0,1:T(8,128)S(1)} all-reduce(f32[16,3,55]{2,0,1:T(8,128)S(1)} %fusion.8), channel_id=2, replica_groups=mesh['vert'=8,'col'=4] {'vert'}, use_global_device_ids=true, to_apply=%region_0.0.clone | all-reduce | flops 2640 | bytes 21120
  73.6 0.7 copy-done.8
  77.1 169.4 %while.19 = (s32[]{:T(128)}, f32[55,3,3,2]{2,3,1,0:T(2,128)S(1)}, f32[55,3,2]{1,2,0:T(2,128)S(1)}, f32[55,3,3,2]{2,3,1,0:T(2,128)S(1)}, s32[55]{0:T(128)S(1)}, /...) while((s32[]{:T(128)}, f32[55,3,3,2]{2,3,1,0:T(2,128)S(1)}, ...), condition=%wide.region_2.0_spmd, body=%wide.region_1.0_spmd.sunk | while | flops 884 | bytes 9465 | solution.py:58
  80.2 0.7 dynamic_slice.89
  83.3 0.7 dynamic_slice.89
  86.5 0.6 dynamic_slice.89
  89.6 0.7 dynamic_slice.89
  92.7 0.6 dynamic_slice.89
  95.9 0.7 dynamic_slice.89
  99.0 0.6 dynamic_slice.89
  102.2 0.7 dynamic_slice.89
  105.3 0.7 dynamic_slice.89
  108.4 0.6 dynamic_slice.89
  111.6 0.7 dynamic_slice.89
  114.7 0.6 dynamic_slice.89
  117.8 0.7 dynamic_slice.89
  121.0 0.6 dynamic_slice.89
  124.1 0.7 dynamic_slice.89
  127.3 0.7 dynamic_slice.89
  130.4 0.7 dynamic_slice.89
  133.5 0.7 dynamic_slice.89
  136.7 0.6 dynamic_slice.89
  139.8 0.7 dynamic_slice.89
  142.9 0.6 dynamic_slice.89
  146.1 0.7 dynamic_slice.89
  149.2 0.6 dynamic_slice.89
  152.4 0.7 dynamic_slice.89
  155.5 0.7 dynamic_slice.89
  158.6 0.6 dynamic_slice.89
  161.8 0.7 dynamic_slice.89
  164.9 0.6 dynamic_slice.89
  168.0 0.7 dynamic_slice.89
  171.2 0.6 dynamic_slice.89
  174.3 0.7 dynamic_slice.89
  177.5 0.7 dynamic_slice.89
  180.6 0.7 dynamic_slice.89
  183.7 0.7 dynamic_slice.89
  186.9 0.6 dynamic_slice.89
  190.0 0.7 dynamic_slice.89
  193.1 0.6 dynamic_slice.89
  196.3 0.7 dynamic_slice.89
  199.4 0.6 dynamic_slice.89
  202.6 0.7 dynamic_slice.89
  205.7 0.7 dynamic_slice.89
  208.8 0.6 dynamic_slice.89
  212.0 0.7 dynamic_slice.89
  215.1 0.6 dynamic_slice.89
  218.2 0.7 dynamic_slice.89
  221.4 0.6 dynamic_slice.89
  224.5 0.7 dynamic_slice.89
  227.7 0.7 dynamic_slice.89
  230.8 0.7 dynamic_slice.89
  233.9 0.7 dynamic_slice.89
  237.1 0.6 dynamic_slice.89
  240.2 0.7 dynamic_slice.89
  243.3 0.6 dynamic_slice.89
  247.3 30.5 %all_gather.11 = f32[16,12,55]{2,1,0:T(8,128)S(1)} all-gather(f32[2,12,55]{2,1,0:T(8,128)S(1)} %copy.95), channel_id=1, replica_groups=mesh['vert'=8,'col'=4] {'vert'}, dimensions={0}, use_global_device_ids=true | all-gather | bytes 47520 | tf_op jit(solution)/shard_map/all_gather | solution.py:121
  277.9 0.7 copy-done.4
  279.0 8.9 %all_to_all.18 = bf16[8,2,246]{2,1,0:T(2,128)(2,1)S(1)} all-to-all(bf16[8,2,246]{2,1,0:T(2,128)(2,1)S(1)} %reshape.121), channel_id=1, replica_groups=mesh['vert'=8,'col'=4] {'vert'}, dimensions={0} | all-to-all | bytes 15744 | tf_op jit(solution)/shard_map/all_to_all | solution.py:125
  288.0 0.7 all_to_all.16
  (543 shorter events, 38.0 us)
Async XLA Ops:
  0.0 38.0 %copy-start = (f32[55,82]{1,0:T(8,128)S(1)}, f32[55,82]{1,0:T(8,128)}, u32[]{:S(2)}) copy-start(f32[55,82]{1,0:T(8,128)} %param.18) | copy-start | bytes 54124
  0.0 0.9 copy-start.2
  0.0 29.8 %copy-start.1 = (bf16[100,3,82]{0,2,1:T(8,128)(2,1)S(1)}, bf16[100,3,82]{0,2,1:T(8,128)(2,1)}, u32[]{:S(2)}) copy-start(bf16[100,3,82]{0,2,1:T(8,128)(2,1)} %param.16) | copy-start | bytes 147604
  37.0 0.7 copy-start.6
  73.6 0.7 copy-start.8
  75.7 0.7 copy-start.5
  76.4 0.7 copy-start.7
  247.3 30.6 %copy-start.3 = (f32[82,4]{0,1:T(4,128)S(1)}, f32[82,4]{0,1:T(4,128)}, u32[]{:S(2)}) copy-start(f32[82,4]{0,1:T(4,128)} %param.23) | copy-start | bytes 3940
  277.9 0.7 copy-start.4
where the time goes:
time: 291 us; the launch traced here: 289 us
  blocking collectives  109 us (37%)
  loops' own time  102 us (35%)
  local copies, waits for them, and re-layouts  54.8 us (19%)
  matrix products  19.3 us (7%)
    another operation x1, loops' own time, kinematics(): lax.fori_loop(1, joint_total, compose, (glob_rot, glob_pos))  102 us
    unnamed x1, blocking collectives  35.4 us
    dynamic_slice x54, local copies, waits for them, and re-layouts, compose(): parent = lax.dynamic_index_in_dim(parents, joint, 0, keepdims=False)  35.1 us
    all_gather x1, blocking collectives, body(): group_frames = lax.all_gather(own_frames, 'vert', axis=0, tiled=True)  30.5 us
    all_gather x1, blocking collectives, body(): lax.all_gather(coeffs, 'vert', axis=0, tiled=True)  28.1 us
    dot_general x54, matrix products, compose(): jnp.einsum('amc,mbc->abc', parent_rot, local_rot, precision=lax.Precision...  11.1 us
    all_to_all x1, blocking collectives, body(): lax.all_to_all(posed_local, 'vert', split_axis=0, concat_axis=2, tiled=True)  8.89 us
    dot_general x54, matrix products, compose(): jnp.einsum('amc,mc->ac', parent_rot, offset, precision=lax.Precision.HIGH...  7.68 us

commit v1 on v0

--- a/solution.py
+++ b/solution.py
@@ -118,9 +118,25 @@
     )
     joints = lax.psum_scatter(partial_value, "vert", scatter_dimension=0, tiled=True)
     own_frames = kinematics(joints, quaternions, translation, parents)
-    group_frames = lax.all_gather(own_frames, "vert", axis=0, tiled=True)
     weight_grid = dense_weights(skin_index, skin_raw, joint_total)
-    blended = jnp.einsum("cej,jv->cev", group_frames, weight_grid, precision=lax.Precision.HIGHEST)
+    new = jax.lax.axis_index("vert")
+    side_arr = jax.lax.axis_size("vert")
+    z2, then, h_now = (side_arr, new, own_frames.shape[0])
+    cards = [(hop_no, (hop_no + 1) % z2) for hop_no in range(z2)]
+    block_now, blended = (own_frames, None)
+    for p in range(z2):
+        arr_next = (then - p) % z2
+        next_value = (
+            jax.lax.ppermute(block_now, axis_name="vert", perm=cards) if p < z2 - 1 else None
+        )
+        small = jnp.einsum("cej,jv->cev", block_now, weight_grid, precision=lax.Precision.HIGHEST)
+        parts_out = small.shape[0]
+        if blended is None:
+            blended = jnp.zeros(
+                (*small.shape[:0], z2 * parts_out, *small.shape[0 + 1 :]), small.dtype
+            )
+        blended = lax.dynamic_update_slice_in_dim(blended, small, arr_next * parts_out, axis=0)
+        block_now = next_value
     posed_local = apply_frames(blended, shaped_three.astype(jnp.float32)).astype(jnp.bfloat16)
     return lax.all_to_all(posed_local, "vert", split_axis=0, concat_axis=2, tiled=True)
 

time: 291 us -> 287 us (0.986)
  waiting for transfers between devices: 0 us -> 42.4 us
  blocking collectives: 109 us -> 78.9 us
  loops' own time: 102 us -> 89.4 us
  local copies, waits for them, and re-layouts: 54.8 us -> 51.4 us
    ppermute x0 -> x7, waiting for transfers between devices: none -> 42.4 us  [body(): jax.lax.ppermute(block_now, axis_name='vert', perm=cards)]
    all_gather x1 -> x0, blocking collectives: 30.5 us -> none  [body(): group_frames = lax.all_gather(own_frames, 'vert', axis=0, tiled=True)]
    another operation x1, loops' own time: 102 us -> 89.4 us  [kinematics(): lax.fori_loop(1, joint_total, compose, (glob_rot, glob_pos))]
    dynamic_slice x54, local copies, waits for them, and re-layouts: 35.1 us -> 30.7 us  [compose(): parent = lax.dynamic_index_in_dim(parents, joint, 0, keepdims=False)]
    unnamed x25 -> x29, local copies, waits for them, and re-layouts: 4.25 us -> 5.93 us
  transfers between devices with their start and end apart: 0 -> 7, of which waited for: 0 -> 7; matrix products, arithmetic and copies ran while one was open for 0% -> 0% of each run, Pallas kernels for 0% -> 0%
where the time goes in v1:
time: 287 us; the launch traced here: 285 us
  loops' own time  89.4 us (31%)
  blocking collectives  78.9 us (27%)
  local copies, waits for them, and re-layouts  51.4 us (18%)
  waiting for transfers between devices  42.4 us (15%)
  matrix products  20.2 us (7%)
    another operation x1, loops' own time, kinematics(): lax.fori_loop(1, joint_total, compose, (glob_rot, glob_pos))  89.4 us
    ppermute x7, waiting for transfers between devices, body(): jax.lax.ppermute(block_now, axis_name='vert', perm=cards)  42.4 us
    unnamed x1, blocking collectives  35.6 us
    dynamic_slice x54, local copies, waits for them, and re-layouts, compose(): parent = lax.dynamic_index_in_dim(parents, joint, 0, keepdims=False)  30.7 us
    all_gather x1, blocking collectives, body(): lax.all_gather(coeffs, 'vert', axis=0, tiled=True)  27.9 us
    dot_general x54, matrix products, compose(): jnp.einsum('amc,mbc->abc', parent_rot, local_rot, precision=lax.Precision...  11.1 us
    all_to_all x1, blocking collectives, body(): lax.all_to_all(posed_local, 'vert', split_axis=0, concat_axis=2, tiled=True)  8.89 us
    dot_general x54, matrix products, compose(): jnp.einsum('amc,mc->ac', parent_rot, offset, precision=lax.Precision.HIGH...  7.68 us
  transfers between devices with their start and end apart: 7, of which 7 were waited for; matrix products, arithmetic and copies ran while one was open for 0% of the time, Pallas kernels for 0%

profile of v1, /device:TPU:0, one launch (start us, length us, event | category | flops | bytes accessed | tf_op | source)
XLA Modules:
  0.0 285.4 jit_solution(461130200804928822)
XLA Ops:
  0.0 0.9 multiply_add_fusion.2
  1.0 0.6 copy-done.8
  2.4 0.6 copy-done.4
  3.0 27.9 %all-gather = bf16[8,2,400]{2,1,0:T(2,128)(2,1)S(1)} all-gather(bf16[1,2,400]{2,1,0:T(2,128)(2,1)S(1)} %bitcast.182), channel_id=1, replica_groups=mesh['vert'=8,'col'=4] {'vert'}, dimensions={0}, use_global_device_ids=true | all-gather | bytes 14400 | tf_op jit(solution)/shard_map/all_gather | solution.py:105
  31.1 6.5 %all_gather.7 = bf16[400,3,82]{2,1,0:T(4,128)(2,1)S(1)} all-gather(bf16[100,3,82]{2,1,0:T(4,128)(2,1)S(1)} %copy.56), channel_id=1, replica_groups=mesh['vert'=8,'col'=4] {'col'}, dimensions={0}, use_global_device_ids=true | all-gather | bytes 246000 | tf_op jit(solution)/shard_map/all_gather | solution.py:98
  38.3 35.6 %all-reduce.1 = f32[16,3,55]{2,0,1:T(8,128)S(1)} all-reduce(f32[16,3,55]{2,0,1:T(8,128)S(1)} %fusion.13), channel_id=2, replica_groups=mesh['vert'=8,'col'=4] {'vert'}, use_global_device_ids=true, to_apply=%region_0.0.clone | all-reduce | flops 2640 | bytes 21120
  73.9 0.7 copy-done.10
  76.6 0.6 copy-done.9
  77.2 152.1 %while.19 = (s32[]{:T(128)}, f32[55,3,3,2]{2,3,1,0:T(2,128)S(1)}, f32[55,3,2]{1,2,0:T(2,128)S(1)}, f32[55,3,3,2]{2,3,1,0:T(2,128)S(1)}, s32[55]{0:T(128)S(1)}, /...) while((s32[]{:T(128)}, f32[55,3,3,2]{2,3,1,0:T(2,128)S(1)}, ...), condition=%wide.region_2.0_spmd, body=%wide.region_1.0_spmd.sunk | while | flops 884 | bytes 9465 | solution.py:58
  80.0 0.6 dynamic_slice.89
  82.8 0.6 dynamic_slice.89
  88.5 0.6 dynamic_slice.89
  91.3 0.6 dynamic_slice.89
  94.1 0.6 dynamic_slice.89
  96.9 0.6 dynamic_slice.89
  99.7 0.6 dynamic_slice.89
  102.6 0.6 dynamic_slice.89
  105.4 0.6 dynamic_slice.89
  108.2 0.6 dynamic_slice.89
  113.8 0.6 dynamic_slice.89
  116.6 0.6 dynamic_slice.89
  119.5 0.6 dynamic_slice.89
  122.3 0.6 dynamic_slice.89
  125.1 0.6 dynamic_slice.89
  127.9 0.6 dynamic_slice.89
  133.5 0.6 dynamic_slice.89
  136.4 0.6 dynamic_slice.89
  139.2 0.6 dynamic_slice.89
  142.0 0.6 dynamic_slice.89
  144.8 0.6 dynamic_slice.89
  147.6 0.6 dynamic_slice.89
  150.4 0.6 dynamic_slice.89
  153.2 0.6 dynamic_slice.89
  158.9 0.6 dynamic_slice.89
  161.7 0.6 dynamic_slice.89
  164.5 0.6 dynamic_slice.89
  167.3 0.6 dynamic_slice.89
  170.1 0.6 dynamic_slice.89
  173.0 0.6 dynamic_slice.89
  178.6 0.6 dynamic_slice.89
  184.2 0.6 dynamic_slice.89
  187.0 0.6 dynamic_slice.89
  189.9 0.6 dynamic_slice.89
  192.7 0.6 dynamic_slice.89
  195.5 0.6 dynamic_slice.89
  198.3 0.6 dynamic_slice.89
  203.9 0.6 dynamic_slice.89
  206.8 0.6 dynamic_slice.89
  209.6 0.6 dynamic_slice.89
  212.4 0.6 dynamic_slice.89
  215.2 0.6 dynamic_slice.89
  218.0 0.6 dynamic_slice.89
  223.7 0.6 dynamic_slice.89
  230.2 0.7 copy-done.3
  231.0 0.7 copy-done.5
  232.1 4.6 %collective-permute-done = f32[2,12,55]{2,1,0:T(8,128)S(1)} collective-permute-done((f32[2,12,55]{2,1,0:T(8,128)S(1)}, f32[2,12,55]{2,1,0:T(8,128)S(1)}, u32[]{:S(2)}, u32[]{:S(2)}) %collective-permute-start) | collective-permute-done | bytes 5312 | tf_op jit(solution)/shard_map/ppermute | solution.py:130
  236.7 6.3 %collective-permute-done.1 = f32[2,12,55]{2,1,0:T(8,128)S(1)} collective-permute-done((f32[2,12,55]{2,1,0:T(8,128)S(1)}, f32[2,12,55]{2,1,0:T(8,128)S(1)}, u32[]{:S(2)}, u32[]{:S(2)}) %collective-permute-start.1) | collective-permute-done | bytes 5312 | tf_op jit(solution)/shard_map/ppermute | solution.py:130
  243.2 6.3 %collective-permute-done.2 = f32[2,12,55]{2,1,0:T(8,128)S(1)} collective-permute-done((f32[2,12,55]{2,1,0:T(8,128)S(1)}, f32[2,12,55]{2,1,0:T(8,128)S(1)}, u32[]{:S(2)}, u32[]{:S(2)}) %collective-permute-start.2) | collective-permute-done | bytes 5312 | tf_op jit(solution)/shard_map/ppermute | solution.py:130
  249.6 6.3 %collective-permute-done.3 = f32[2,12,55]{2,1,0:T(8,128)S(1)} collective-permute-done((f32[2,12,55]{2,1,0:T(8,128)S(1)}, f32[2,12,55]{2,1,0:T(8,128)S(1)}, u32[]{:S(2)}, u32[]{:S(2)}) %collective-permute-start.3) | collective-permute-done | bytes 5312 | tf_op jit(solution)/shard_map/ppermute | solution.py:130
  256.1 6.3 %collective-permute-done.4 = f32[2,12,55]{2,1,0:T(8,128)S(1)} collective-permute-done((f32[2,12,55]{2,1,0:T(8,128)S(1)}, f32[2,12,55]{2,1,0:T(8,128)S(1)}, u32[]{:S(2)}, u32[]{:S(2)}) %collective-permute-start.4) | collective-permute-done | bytes 5312 | tf_op jit(solution)/shard_map/ppermute | solution.py:130
  262.5 6.3 %collective-permute-done.5 = f32[2,12,55]{2,1,0:T(8,128)S(1)} collective-permute-done((f32[2,12,55]{2,1,0:T(8,128)S(1)}, f32[2,12,55]{2,1,0:T(8,128)S(1)}, u32[]{:S(2)}, u32[]{:S(2)}) %collective-permute-start.5) | collective-permute-done | bytes 5312 | tf_op jit(solution)/shard_map/ppermute | solution.py:130
  268.9 6.3 %collective-permute-done.6 = f32[2,12,55]{2,1,0:T(8,128)S(1)} collective-permute-done((f32[2,12,55]{2,1,0:T(8,128)S(1)}, f32[2,12,55]{2,1,0:T(8,128)S(1)}, u32[]{:S(2)}, u32[]{:S(2)}) %collective-permute-start.6) | collective-permute-done | bytes 5312 | tf_op jit(solution)/shard_map/ppermute | solution.py:130
  275.7 8.9 %all_to_all.18 = bf16[8,2,246]{2,1,0:T(2,128)(2,1)S(1)} all-to-all(bf16[8,2,246]{2,1,0:T(2,128)(2,1)S(1)} %reshape.121), channel_id=1, replica_groups=mesh['vert'=8,'col'=4] {'vert'}, dimensions={0} | all-to-all | bytes 15744 | tf_op jit(solution)/shard_map/all_to_all | solution.py:141
  284.7 0.7 all_to_all.16
  (567 shorter events, 43.3 us)
Async XLA Ops:
  0.0 38.1 %copy-start = (f32[55,82]{1,0:T(8,128)S(1)}, f32[55,82]{1,0:T(8,128)}, u32[]{:S(2)}) copy-start(f32[55,82]{1,0:T(8,128)} %param.18) | copy-start | bytes 54124
  0.0 0.9 copy-start.2
  1.0 0.7 copy-start.8
  1.7 0.7 copy-start.6
  1.7 29.3 %copy-start.1 = (bf16[100,3,82]{0,2,1:T(8,128)(2,1)S(1)}, bf16[100,3,82]{0,2,1:T(8,128)(2,1)}, u32[]{:S(2)}) copy-start(bf16[100,3,82]{0,2,1:T(8,128)(2,1)} %param.16) | copy-start | bytes 147604
  2.3 0.7 copy-start.4
  73.9 0.7 copy-start.10
  75.9 0.7 copy-start.7
  76.6 0.7 copy-start.9
  230.1 6.5 %collective-permute-start = (f32[2,12,55]{2,1,0:T(8,128)S(1)}, f32[2,12,55]{2,1,0:T(8,128)S(1)}, u32[]{:S(2)}, u32[]{:S(2)}) collective-permute-start(f32[2,12,55]{2,1,0:T(8,128)S(1)} %maximum_bitcast_fusion), channel_id=1, source_target_pairs={{0,4},{4,8},{8,12},{12,16},{16,20},{20,24},{24,28},{28,0},{1,5},{5... | collective-permute-start | bytes 15848 | tf_op jit(solution)/shard_map/ppermute | solution.py:130
  230.2 0.7 copy-start.3
  230.9 0.7 copy-start.5
  236.6 6.4 %collective-permute-start.1 = (f32[2,12,55]{2,1,0:T(8,128)S(1)}, f32[2,12,55]{2,1,0:T(8,128)S(1)}, u32[]{:S(2)}, u32[]{:S(2)}) collective-permute-start(f32[2,12,55]{2,1,0:T(8,128)S(1)} %collective-permute-done), channel_id=1, source_target_pairs={{0,4},{4,8},{8,12},{12,16},{16,20},{20,24},{24,28},{28,0},{1,5},{5... | collective-permute-start | bytes 15848 | tf_op jit(solution)/shard_map/ppermute | solution.py:130
  243.0 6.4 %collective-permute-start.2 = (f32[2,12,55]{2,1,0:T(8,128)S(1)}, f32[2,12,55]{2,1,0:T(8,128)S(1)}, u32[]{:S(2)}, u32[]{:S(2)}) collective-permute-start(f32[2,12,55]{2,1,0:T(8,128)S(1)} %collective-permute-done.1), channel_id=1, source_target_pairs={{0,4},{4,8},{8,12},{12,16},{16,20},{20,24},{24,28},{28,0},{1,5},{5... | collective-permute-start | bytes 15848 | tf_op jit(solution)/shard_map/ppermute | solution.py:130
  249.5 6.4 %collective-permute-start.3 = (f32[2,12,55]{2,1,0:T(8,128)S(1)}, f32[2,12,55]{2,1,0:T(8,128)S(1)}, u32[]{:S(2)}, u32[]{:S(2)}) collective-permute-start(f32[2,12,55]{2,1,0:T(8,128)S(1)} %collective-permute-done.2), channel_id=1, source_target_pairs={{0,4},{4,8},{8,12},{12,16},{16,20},{20,24},{24,28},{28,0},{1,5},{5... | collective-permute-start | bytes 15848 | tf_op jit(solution)/shard_map/ppermute | solution.py:130
  255.9 6.4 %collective-permute-start.4 = (f32[2,12,55]{2,1,0:T(8,128)S(1)}, f32[2,12,55]{2,1,0:T(8,128)S(1)}, u32[]{:S(2)}, u32[]{:S(2)}) collective-permute-start(f32[2,12,55]{2,1,0:T(8,128)S(1)} %collective-permute-done.3), channel_id=1, source_target_pairs={{0,4},{4,8},{8,12},{12,16},{16,20},{20,24},{24,28},{28,0},{1,5},{5... | collective-permute-start | bytes 15848 | tf_op jit(solution)/shard_map/ppermute | solution.py:130
  262.4 6.5 %collective-permute-start.5 = (f32[2,12,55]{2,1,0:T(8,128)S(1)}, f32[2,12,55]{2,1,0:T(8,128)S(1)}, u32[]{:S(2)}, u32[]{:S(2)}) collective-permute-start(f32[2,12,55]{2,1,0:T(8,128)S(1)} %collective-permute-done.4), channel_id=1, source_target_pairs={{0,4},{4,8},{8,12},{12,16},{16,20},{20,24},{24,28},{28,0},{1,5},{5... | collective-permute-start | bytes 15848 | tf_op jit(solution)/shard_map/ppermute | solution.py:130
  268.8 6.4 %collective-permute-start.6 = (f32[2,12,55]{2,1,0:T(8,128)S(1)}, f32[2,12,55]{2,1,0:T(8,128)S(1)}, u32[]{:S(2)}, u32[]{:S(2)}) collective-permute-start(f32[2,12,55]{2,1,0:T(8,128)S(1)} %collective-permute-done.5), channel_id=1, source_target_pairs={{0,4},{4,8},{8,12},{12,16},{16,20},{20,24},{24,28},{28,0},{1,5},{5... | collective-permute-start | bytes 15848 | tf_op jit(solution)/shard_map/ppermute | solution.py:130
